TPU v7x, 128 devices: a whole 4x4x4 slice. The times are simulated.
128 devices in a mesh: dp: 16 (over y, z_lo, core), ep: 8 (over z_hi, x).
Axes of the slice: x: 4, y: 4, z: 4 (z_hi: 2, z_lo: 2; z = z_hi * 2 + z_lo), core: 2. Of those that a mesh axis runs over, the one named last changes fastest.
Arguments:
- tokens: bfloat16 [16384, 6144], P(('dp', 'ep')), may hold values from -6 to 6
- out_grad: bfloat16 [16384, 6144], P(('dp', 'ep')), may hold values from -0.75 to 0.75
- expert_ids: int32 [16384, 2], P(('dp', 'ep')), may hold values from 0 to 7, all different within a row; in each aligned block of 128 rows (0 to 127, 128 to 255, ...) at most 40 rows name the same one
- route_weight: float32 [16384, 2], P(('dp', 'ep')), may hold values from 0.2 to 1
- w_gate: bfloat16 [8, 6144, 256], P('ep', 'dp'), may hold values from -0.078125 to 0.078125
- w_up: bfloat16 [8, 6144, 256], P('ep', 'dp'), may hold values from -0.078125 to 0.078125
- w_down: bfloat16 [8, 256, 6144], P('ep', None, 'dp'), may hold values from -0.375 to 0.375
Outputs:
- d_tokens: bfloat16 [16384, 6144], P(('dp', 'ep'))
- grad_gate: float32 [8, 6144, 256], P('ep', 'dp')
- grad_up: float32 [8, 6144, 256], P('ep', 'dp')
- grad_down: float32 [8, 256, 6144], P('ep', None, 'dp')
Inputs may be any that keep to these rules, and one draw needn't show every extreme that they name: `expert_ids`: each token names two different experts. Among the 128 tokens of one device (aligned blocks of 128 rows) no expert is named more than 40 times, and in some blocks one expert is named exactly 40 times.
All inputs are finite; a program needn't handle non-finite values.
Results may differ from a plain program's by a relative error of at most 0.0065.
Values may be sent and summed in bfloat16 or wider, within the bound.
A program may use at most 128 MiB of HBM per device.

v0:
```python
import jax
import jax.numpy as jnp
from jax import lax
from jax.sharding import PartitionSpec as P


def in_one_piece(arrays, axis, dim, along):
    widths = [a.shape[along] for a in arrays]
    both = jnp.concatenate(arrays, axis=along)
    result = lax.all_gather(both, axis, axis=dim, tiled=True)
    return tuple(jnp.split(result, [sum(widths[:k]) for k in range(1, len(widths))], axis=along))


def contract_rows(left, right):
    return lax.dot_general(
        left, right, (((0,), (0,)), ((), ())), preferred_element_type=jnp.float32
    )


def contract_last(left, right):
    return lax.dot_general(
        left, right, (((1,), (1,)), ((), ())), preferred_element_type=jnp.float32
    )


def shards(tokens, out_grad, expert_ids, route_weight, w_gate, w_up, w_down):
    tok_dev, width = tokens.shape
    experts = lax.axis_size("ep")
    capacity = 10 * tok_dev // (4 * experts)
    flat_ids = expert_ids.reshape(-1)
    onehot = (flat_ids[:, None] == jnp.arange(experts, dtype=jnp.int32)).astype(jnp.int32)
    slot_rank = jnp.sum((jnp.cumsum(onehot, axis=0) - onehot) * onehot, axis=1)
    slot_index = flat_ids * capacity + slot_rank
    pair_rows = jnp.repeat(tokens, 2, axis=0)
    scaled = (
        route_weight.reshape(-1)[:, None] * jnp.repeat(out_grad, 2, axis=0).astype(jnp.float32)
    ).astype(jnp.bfloat16)
    empty = jnp.zeros((experts * capacity, width), jnp.bfloat16)
    send_rows = empty.at[slot_index].set(pair_rows).reshape(experts, capacity, width)
    send_scaled = empty.at[slot_index].set(scaled).reshape(experts, capacity, width)
    recv_rows, recv_scaled = (
        lax.all_to_all(send_rows, "ep", split_axis=0, concat_axis=0, tiled=True),
        lax.all_to_all(send_scaled, "ep", split_axis=0, concat_axis=0, tiled=True),
    )
    x_rows = recv_rows.reshape(-1, width)
    grad_out = recv_scaled.reshape(-1, width)
    gate_w, up_w = in_one_piece((w_gate[0], w_up[0]), "dp", 0, 1)
    gate_pre = jnp.dot(x_rows, gate_w, preferred_element_type=jnp.float32)
    up_pre = jnp.dot(x_rows, up_w, preferred_element_type=jnp.float32)
    grad_hidden = contract_last(grad_out, lax.all_gather(w_down[0], "dp", axis=1, tiled=True))
    sigmoid_a = jax.nn.sigmoid(gate_pre)
    silu_a = gate_pre * sigmoid_a
    hidden = (silu_a * up_pre).astype(jnp.bfloat16)
    grad_gate_pre = (
        grad_hidden * up_pre * sigmoid_a * (1.0 + gate_pre * (1.0 - sigmoid_a))
    ).astype(jnp.bfloat16)
    grad_up_pre = (grad_hidden * silu_a).astype(jnp.bfloat16)
    pair_grad = (contract_last(grad_gate_pre, gate_w) + contract_last(grad_up_pre, up_w)).astype(
        jnp.bfloat16
    )
    back = lax.all_to_all(
        pair_grad.reshape(experts, capacity, width), "ep", split_axis=0, concat_axis=0, tiled=True
    )
    picked = back.reshape(-1, width)[slot_index].reshape(tok_dev, 2, width)
    d_tokens = jnp.sum(picked.astype(jnp.float32), axis=1).astype(jnp.bfloat16)
    column_rows, column_grad = (
        lax.all_to_all(x_rows, "dp", split_axis=1, concat_axis=0, tiled=True),
        lax.all_to_all(grad_out, "dp", split_axis=1, concat_axis=0, tiled=True),
    )
    every_gate, every_up, every_hidden = in_one_piece(
        (grad_gate_pre, grad_up_pre, hidden), "dp", 0, 1
    )
    shard_gate = contract_rows(column_rows, every_gate)
    shard_up = contract_rows(column_rows, every_up)
    shard_down = contract_rows(column_grad, every_hidden)
    return (d_tokens, shard_gate[None], shard_up[None], jnp.transpose(shard_down)[None])


def solution(mesh):
    in_specs = (
        P(("dp", "ep"), None),
        P(("dp", "ep"), None),
        P(("dp", "ep"), None),
        P(("dp", "ep"), None),
        P("ep", "dp", None),
        P("ep", "dp", None),
        P("ep", None, "dp"),
    )
    out_specs = (
        P(("dp", "ep"), None),
        P("ep", "dp", None),
        P("ep", "dp", None),
        P("ep", None, "dp"),
    )
    return jax.shard_map(shards, mesh=mesh, in_specs=in_specs, out_specs=out_specs, check_vma=False)
```

profile of v0, /device:TPU:55, one launch (start us, length us, event | category | flops | bytes accessed | tf_op | source)
XLA Modules:
  0.0 404.8 jit_solution(12341281554003499555)
XLA Ops:
  7.2 0.7 all-gather.9.cloned.1.call-update
  7.9 0.0 all-gather.5.cloned.1.call-start
  7.9 1.8 pad_maximum_fusion.1
  9.8 0.8 copy.22
  10.6 0.1 eq.29
  10.7 0.1 eq.25
  10.8 0.6 reduce-window.6
  11.4 0.2 slice_reduce_fusion
  11.7 0.7 broadcast_multiply_fusion
  12.4 0.1 copy.21
  12.5 0.1 mul.52
  12.6 6.8 %broadcast_in_dim.23 = f32[128,2,6144]{2,1,0:T(2,128)} broadcast(bf16[128,6144]{1,0:T(8,128)(2,1)} %param.8), dimensions={0,2} | broadcast | bytes 7864320 | tf_op jit(solution)/shard_map/broadcast_in_dim | solution.py:36
  19.5 8.4 %convert_element_type.34 = f32[256,6144]{1,0:T(8,128)} reshape(f32[128,2,6144]{2,1,0:T(2,128)} %broadcast_in_dim.23) | data formatting | bytes 12582912 | tf_op jit(solution)/shard_map/convert_element_type | solution.py:36
  27.9 0.1 copy.24
  28.0 0.1 mul.54
  28.1 0.1 fusion.32
  28.2 9.5 %scatter_custom_fusion = bf16[320,6144]{1,0:T(8,128)(2,1)} fusion(s32[256]{0:T(256)S(1)} %bitcast.56, f32[256,6144]{1,0:T(8,128)} %convert_element_type.34, f32[256]{0:T(256)S(1)} %mul.54, bf16[]{:T(256)} %constant.5.clone.1), kind=kCustom, calls=%fused_computation.6 | custom fusion | flops 3145728 | bytes 10224642 | tf_op jit(solution)/shard_map/scatter | solution.py:40
  37.7 7.3 %all-to-all-start = ((bf16[8,40,6144]{2,1,0:T(8,128)(2,1)}), bf16[8,40,6144]{2,1,0:T(8,128)(2,1)}, u32[]{:S(2)}, u32[]{:S(2)}) async-start(bf16[8,40,6144]{2,1,0:T(8,128)(2,1)} %bitcast.49), calls=%async_computation | async-start | bytes 7864320 | tf_op jit(solution)/shard_map/all_to_all | solution.py:43
  45.0 3.3 broadcast_in_dim.24
  48.3 2.7 reshape.118
  51.0 8.4 %scatter_custom_fusion.1 = bf16[320,6144]{1,0:T(8,128)(2,1)} fusion(s32[256]{0:T(256)S(1)} %bitcast.57, bf16[256,6144]{1,0:T(8,128)(2,1)} %reshape.118, bf16[]{:T(256)} %constant.5.clone.1), kind=kCustom, calls=%fused_computation.23 | custom fusion | bytes 3932672 | tf_op jit(solution)/shard_map/scatter | solution.py:39
  59.5 42.4 %all-to-all-done = bf16[8,40,6144]{2,1,0:T(8,128)(2,1)} async-done(((bf16[8,40,6144]{2,1,0:T(8,128)(2,1)}), bf16[8,40,6144]{2,1,0:T(8,128)(2,1)}, u32[]{:S(2)}, u32[]{:S(2)}) %all-to-all-start) | async-done | bytes 3932192 | tf_op jit(solution)/shard_map/all_to_all | solution.py:43
  101.9 6.4 %all-to-all-start.1 = ((bf16[8,40,6144]{2,1,0:T(8,128)(2,1)}), bf16[8,40,6144]{2,1,0:T(8,128)(2,1)}, u32[]{:S(2)}, u32[]{:S(2)}) async-start(bf16[8,40,6144]{2,1,0:T(8,128)(2,1)} %bitcast.48), calls=%async_computation.1 | async-start | bytes 7864320 | tf_op jit(solution)/shard_map/all_to_all | solution.py:42
  108.3 0.2 all-gather.7.cloned.1.call-start
  108.5 4.4 %fusion.2 = f32[320,256]{1,0:T(8,128)S(1)} fusion(bf16[320,6144]{1,0:T(8,128)(2,1)} %bitcast.5, bf16[1,256,6144]{2,1,0:T(8,128)(2,1)} %all-gather.9.cloned.1.call-done), kind=kOutput, calls=%fused_computation.7 | convolution fusion | flops 1006632960 | bytes 7405568 | tf_op jit(solution)/shard_map/dot_general | solution.py:21
  112.9 47.6 %all-to-all-done.1 = bf16[8,40,6144]{2,1,0:T(8,128)(2,1)} async-done(((bf16[8,40,6144]{2,1,0:T(8,128)(2,1)}), bf16[8,40,6144]{2,1,0:T(8,128)(2,1)}, u32[]{:S(2)}, u32[]{:S(2)}) %all-to-all-start.1) | async-done | bytes 3932192 | tf_op jit(solution)/shard_map/all_to_all | solution.py:42
  160.5 4.4 %fusion.7 = f32[320,256]{1,0:T(8,128)S(1)} fusion(bf16[320,6144]{1,0:T(8,128)(2,1)} %bitcast.8, bf16[6144,512]{1,0:T(8,128)(2,1)} %all-gather.5.cloned.1.call-done), kind=kOutput, calls=%fused_computation.12 | convolution fusion | flops 1006632960 | bytes 7405568 | tf_op jit(solution)/shard_map/dot_general | solution.py:48
  164.9 0.5 copy-done
  165.4 3.3 multiply_convert_fusion.2
  168.7 0.8 pad_maximum_fusion
  169.6 3.0 copy.27
  172.5 2.8 copy.25
  175.4 8.4 %all-to-all-start.3 = ((bf16[320,16,384]{2,0,1:T(8,128)(2,1)}), bf16[320,16,384]{2,0,1:T(8,128)(2,1)}, u32[]{:S(2)}, u32[]{:S(2)}) async-start(bf16[320,16,384]{2,0,1:T(8,128)(2,1)} %copy.25), calls=%async_computation.3 | async-start | bytes 7864320 | tf_op jit(solution)/shard_map/all_to_all | solution.py:67
  183.8 3.3 fusion.5
  187.1 3.2 fusion
  190.3 68.9 %all-to-all-done.3 = bf16[320,16,384]{2,0,1:T(8,128)(2,1)} async-done(((bf16[320,16,384]{2,0,1:T(8,128)(2,1)}), bf16[320,16,384]{2,0,1:T(8,128)(2,1)}, u32[]{:S(2)}, u32[]{:S(2)}) %all-to-all-start.3) | async-done | bytes 3932192 | tf_op jit(solution)/shard_map/all_to_all | solution.py:67
  259.2 6.4 %all-to-all-start.2 = ((bf16[8,40,6144]{2,1,0:T(8,128)(2,1)}), bf16[8,40,6144]{2,1,0:T(8,128)(2,1)}, u32[]{:S(2)}, u32[]{:S(2)}) async-start(bf16[8,40,6144]{2,1,0:T(8,128)(2,1)} %bitcast.47), calls=%async_computation.2 | async-start | bytes 7864320 | tf_op jit(solution)/shard_map/all_to_all | solution.py:61
  265.6 3.0 copy.28
  268.6 2.8 copy.26
  271.4 51.4 %all-to-all-done.2 = bf16[8,40,6144]{2,1,0:T(8,128)(2,1)} async-done(((bf16[8,40,6144]{2,1,0:T(8,128)(2,1)}), bf16[8,40,6144]{2,1,0:T(8,128)(2,1)}, u32[]{:S(2)}, u32[]{:S(2)}) %all-to-all-start.2) | async-done | bytes 3932192 | tf_op jit(solution)/shard_map/all_to_all | solution.py:61
  322.8 14.8 %all-to-all-start.4 = ((bf16[320,16,384]{2,0,1:T(8,128)(2,1)}), bf16[320,16,384]{2,0,1:T(8,128)(2,1)}, u32[]{:S(2)}, u32[]{:S(2)}) async-start(bf16[320,16,384]{2,0,1:T(8,128)(2,1)} %copy.26), calls=%async_computation.4 | async-start | bytes 7864320 | tf_op jit(solution)/shard_map/all_to_all | solution.py:68
  337.6 9.7 %gather_fusion = bf16[256,6144]{1,0:T(8,128)(2,1)} fusion(bf16[320,6144]{1,0:T(8,128)(2,1)} %bitcast.12, s32[1024]{0:T(1024)S(1)} %pad_clamp_fusion), kind=kCustom, calls=%fused_computation | custom fusion | bytes 6292480 | tf_op jit(solution)/shard_map/gather | solution.py:64
  347.3 6.2 %reshape.97 = bf16[128,2,6144]{2,1,0:T(2,128)(2,1)S(1)} reshape(bf16[256,6144]{1,0:T(8,128)(2,1)} %gather_fusion) | data formatting | bytes 6291456 | tf_op jit(solution)/shard_map/reshape | solution.py:64
  353.5 9.7 %reduce_sum.25 = bf16[128,6144]{1,0:T(8,128)(2,1)} reduce(bf16[128,2,6144]{2,1,0:T(2,128)(2,1)S(1)} %reshape.97, bf16[]{:T(256)} %constant.5.clone.1), dimensions={1}, to_apply=%region_5.6 | reduce | flops 786432 | bytes 4718594 | tf_op jit(solution)/shard_map/reduce_sum | solution.py:65
  363.3 4.9 %fusion.24 = f32[1,384,256]{2,1,0:T(8,128)} fusion(bf16[5120,384]{1,0:T(8,128)(2,1)} %bitcast.14, bf16[5120,768]{1,0:T(8,128)(2,1)} %all-gather.7.cloned.1.call-done), kind=kOutput, calls=%fused_computation.27 | convolution fusion | flops 1006632960 | bytes 6946816 | tf_op jit(solution)/shard_map/dot_general | solution.py:15
  368.2 4.9 %fusion.21 = f32[1,384,256]{2,1,0:T(8,128)} fusion(bf16[5120,384]{1,0:T(8,128)(2,1)} %bitcast.14, bf16[5120,768]{1,0:T(8,128)(2,1)} %all-gather.7.cloned.1.call-done), kind=kOutput, calls=%fused_computation.26 | convolution fusion | flops 1006632960 | bytes 6946816 | tf_op jit(solution)/shard_map/dot_general | solution.py:15
  373.1 19.6 %all-to-all-done.4 = bf16[320,16,384]{2,0,1:T(8,128)(2,1)} async-done(((bf16[320,16,384]{2,0,1:T(8,128)(2,1)}), bf16[320,16,384]{2,0,1:T(8,128)(2,1)}, u32[]{:S(2)}, u32[]{:S(2)}) %all-to-all-start.4) | async-done | bytes 3932192 | tf_op jit(solution)/shard_map/all_to_all | solution.py:68
  392.6 5.2 %fusion.27 = f32[1,256,384]{2,1,0:T(8,128)} fusion(bf16[5120,384]{1,0:T(8,128)(2,1)} %bitcast.19, bf16[5120,768]{1,0:T(8,128)(2,1)} %all-gather.7.cloned.1.call-done), kind=kOutput, calls=%fused_computation.28 | convolution fusion | flops 1006632960 | bytes 6946816 | tf_op jit(solution)/shard_map/dot_general | solution.py:15
  (19 shorter events, 0.2 us)
Async XLA Ops:
  7.2 101.3 %all-gather.9.cloned.1.call-start = ((), (), s32[]{:S(2)}) async-start(), calls=%async_computation.7 | async-start | bytes 3342336 | tf_op jit(solution)/shard_map/all_gather | solution.py:50
  7.9 152.6 %all-gather.5.cloned.1.call-start = ((), (), s32[]{:S(2)}) async-start(), calls=%async_computation.5 | async-start | bytes 6684672 | tf_op jit(solution)/shard_map/all_gather | solution.py:10
  19.5 8.4 %copy-start.1 = (f32[128,2]{0,1:T(2,128)S(1)}, f32[128,2]{0,1:T(2,128)}, u32[]{:S(2)}) copy-start(f32[128,2]{0,1:T(2,128)} %param.10) | copy-start | bytes 3076
  37.7 64.2 %all-to-all-start = ((bf16[8,40,6144]{2,1,0:T(8,128)(2,1)}), bf16[8,40,6144]{2,1,0:T(8,128)(2,1)}, u32[]{:S(2)}, u32[]{:S(2)}) async-start(bf16[8,40,6144]{2,1,0:T(8,128)(2,1)} %bitcast.49), calls=%async_computation | async-start | bytes 7864320 | tf_op jit(solution)/shard_map/all_to_all | solution.py:43
  101.9 58.6 %all-to-all-start.1 = ((bf16[8,40,6144]{2,1,0:T(8,128)(2,1)}), bf16[8,40,6144]{2,1,0:T(8,128)(2,1)}, u32[]{:S(2)}, u32[]{:S(2)}) async-start(bf16[8,40,6144]{2,1,0:T(8,128)(2,1)} %bitcast.48), calls=%async_computation.1 | async-start | bytes 7864320 | tf_op jit(solution)/shard_map/all_to_all | solution.py:42
  108.3 255.0 %all-gather.7.cloned.1.call-start = ((), (), s32[]{:S(2)}) async-start(), calls=%async_computation.6 | async-start | bytes 8355840 | tf_op jit(solution)/shard_map/all_gather | solution.py:10
  160.5 4.9 %copy-start = (bf16[6144,512]{1,0:T(8,128)(2,1)S(1)}, bf16[6144,512]{1,0:T(8,128)(2,1)}, u32[]{:S(2)}) copy-start(bf16[6144,512]{1,0:T(8,128)(2,1)} %all-gather.5.cloned.1.call-done) | copy-start | bytes 18874372
  175.4 11.7 %slice-start = ((s8[6291456]{0:T(1024)(128)(4,1)}), s8[2097152]{0:T(1024)(128)(4,1)S(1)}, s32[]{:S(2)}) async-start(s8[6291456]{0:T(1024)(128)(4,1)} %bitcast.52), calls=%async_computation.8 | async-start | bytes 4194304
  175.4 83.8 %all-to-all-start.3 = ((bf16[320,16,384]{2,0,1:T(8,128)(2,1)}), bf16[320,16,384]{2,0,1:T(8,128)(2,1)}, u32[]{:S(2)}, u32[]{:S(2)}) async-start(bf16[320,16,384]{2,0,1:T(8,128)(2,1)} %copy.25), calls=%async_computation.3 | async-start | bytes 7864320 | tf_op jit(solution)/shard_map/all_to_all | solution.py:67
  183.8 3.3 slice-start.1
  259.2 63.6 %all-to-all-start.2 = ((bf16[8,40,6144]{2,1,0:T(8,128)(2,1)}), bf16[8,40,6144]{2,1,0:T(8,128)(2,1)}, u32[]{:S(2)}, u32[]{:S(2)}) async-start(bf16[8,40,6144]{2,1,0:T(8,128)(2,1)} %bitcast.47), calls=%async_computation.2 | async-start | bytes 7864320 | tf_op jit(solution)/shard_map/all_to_all | solution.py:61
  322.8 69.8 %all-to-all-start.4 = ((bf16[320,16,384]{2,0,1:T(8,128)(2,1)}), bf16[320,16,384]{2,0,1:T(8,128)(2,1)}, u32[]{:S(2)}, u32[]{:S(2)}) async-start(bf16[320,16,384]{2,0,1:T(8,128)(2,1)} %copy.26), calls=%async_computation.4 | async-start | bytes 7864320 | tf_op jit(solution)/shard_map/all_to_all | solution.py:68
Sparse Core Ops, SparseCore 0:
  9.6 36.6 all-gather.8
  48.7 85.5 all-gather.4
  169.7 97.7 all-gather.6
where the time goes:
time: 412 us; the launch traced here: 405 us
  waiting for transfers between devices  231 us (56%)
  local copies, waits for them, and re-layouts  59.4 us (14%)
  starting transfers between devices  43.5 us (11%)
  matrix products  33.6 us (8%)
  other arithmetic  23.3 us (6%)
  between operations  14.3 us (3%)
    all_to_all x1, waiting for transfers between devices, shards(): lax.all_to_all(x_rows, 'dp', split_axis=1, concat_axis=0, tiled=True)  68.9 us
    all_to_all x1, waiting for transfers between devices, shards(): lax.all_to_all(pair_grad.reshape(experts, capacity, width), 'ep', split_a...  51.4 us
    all_to_all x1, waiting for transfers between devices, shards(): lax.all_to_all(send_rows, 'ep', split_axis=0, concat_axis=0, tiled=True)  47.6 us
    all_to_all x1, waiting for transfers between devices, shards(): lax.all_to_all(send_scaled, 'ep', split_axis=0, concat_axis=0, tiled=True)  42.4 us
    all_to_all x1, waiting for transfers between devices, shards(): lax.all_to_all(grad_out, 'dp', split_axis=1, concat_axis=0, tiled=True)  19.6 us
    dot_general x3, matrix products, contract_rows(): lax.dot_general(left, right, (((0,), (0,)), ((), ())), preferred_element_...  15 us
    all_to_all x1, starting transfers between devices, shards(): lax.all_to_all(grad_out, 'dp', split_axis=1, concat_axis=0, tiled=True)  14.8 us
    dot_general x3, matrix products, contract_last(): lax.dot_general(left, right, (((1,), (1,)), ((), ())), preferred_element_...  10.9 us
  transfers between devices with their start and end apart: 8, of which 5 were waited for; matrix products, arithmetic and copies ran while one was open for 25% of the time, Pallas kernels for 0%

commit v1 on v0

--- a/solution.py
+++ b/solution.py
@@ -2,6 +2,13 @@
 import jax.numpy as jnp
 from jax import lax
 from jax.sharding import PartitionSpec as P
+
+
+def trade_parts(value, axis, split, join):
+    devices = lax.axis_size(axis)
+    parts = jnp.stack(jnp.split(value, devices, axis=split), axis=0)
+    parts = lax.all_to_all(parts, axis, split_axis=0, concat_axis=0)
+    return jnp.concatenate(parts, axis=join)
 
 
 def in_one_piece(arrays, axis, dim, along):
@@ -64,7 +71,7 @@
     picked = back.reshape(-1, width)[slot_index].reshape(tok_dev, 2, width)
     d_tokens = jnp.sum(picked.astype(jnp.float32), axis=1).astype(jnp.bfloat16)
     column_rows, column_grad = (
-        lax.all_to_all(x_rows, "dp", split_axis=1, concat_axis=0, tiled=True),
+        trade_parts(x_rows, "dp", 1, 0),
         lax.all_to_all(grad_out, "dp", split_axis=1, concat_axis=0, tiled=True),
     )
     every_gate, every_up, every_hidden = in_one_piece(

time: 412 us -> 419 us (1.017)
  local copies, waits for them, and re-layouts: 59.4 us -> 80.5 us
  starting transfers between devices: 43.5 us -> 34.8 us
  waiting for transfers between devices: 231 us -> 225 us
    unnamed x12 -> x26, local copies, waits for them, and re-layouts: 7.33 us -> 29.5 us
    all_to_all x1, starting transfers between devices: 14.8 us -> 7.32 us  [shards(): lax.all_to_all(grad_out, 'dp', split_axis=1, concat_axis=0, tiled=True)]
    all_to_all x1, waiting for transfers between devices: 68.9 us -> 63 us  [trade_parts(): parts = lax.all_to_all(parts, axis, split_axis=0, concat_axis=0)]
  transfers between devices with their start and end apart: 8 -> 8, of which waited for: 5 -> 5; matrix products, arithmetic and copies ran while one was open for 25% -> 30% of each run, Pallas kernels for 0% -> 0%
where the time goes in v1:
time: 419 us; the launch traced here: 411 us
  waiting for transfers between devices  225 us (54%)
  local copies, waits for them, and re-layouts  80.5 us (19%)
  starting transfers between devices  34.8 us (8%)
  matrix products  33.7 us (8%)
  other arithmetic  23.3 us (6%)
  between operations  14.3 us (3%)
    all_to_all x1, waiting for transfers between devices, trade_parts(): parts = lax.all_to_all(parts, axis, split_axis=0, concat_axis=0)  63 us
    all_to_all x1, waiting for transfers between devices, shards(): lax.all_to_all(pair_grad.reshape(experts, capacity, width), 'ep', split_a...  51.3 us
    all_to_all x1, waiting for transfers between devices, shards(): lax.all_to_all(send_rows, 'ep', split_axis=0, concat_axis=0, tiled=True)  47.6 us
    all_to_all x1, waiting for transfers between devices, shards(): lax.all_to_all(send_scaled, 'ep', split_axis=0, concat_axis=0, tiled=True)  42.4 us
    unnamed x26, local copies, waits for them, and re-layouts  29.5 us
    all_to_all x1, waiting for transfers between devices, shards(): lax.all_to_all(grad_out, 'dp', split_axis=1, concat_axis=0, tiled=True)  19.6 us
    dot_general x3, matrix products, contract_rows(): lax.dot_general(left, right, (((0,), (0,)), ((), ())), preferred_element_...  15 us
    dot_general x3, matrix products, contract_last(): lax.dot_general(left, right, (((1,), (1,)), ((), ())), preferred_element_...  11 us
  transfers between devices with their start and end apart: 8, of which 5 were waited for; matrix products, arithmetic and copies ran while one was open for 30% of the time, Pallas kernels for 0%

profile of v1, /device:TPU:55, one launch (start us, length us, event | category | flops | bytes accessed | tf_op | source)
XLA Modules:
  0.0 411.3 jit_solution(16494814187247713524)
XLA Ops:
  7.9 1.8 pad_maximum_fusion.1
  9.8 0.8 copy.21
  12.6 6.8 %broadcast_in_dim.23 = f32[128,2,6144]{2,1,0:T(2,128)} broadcast(bf16[128,6144]{1,0:T(8,128)(2,1)} %param.8), dimensions={0,2} | broadcast | bytes 7864320 | tf_op jit(solution)/shard_map/broadcast_in_dim | solution.py:43
  19.5 8.4 %convert_element_type.34 = f32[256,6144]{1,0:T(8,128)} reshape(f32[128,2,6144]{2,1,0:T(2,128)} %broadcast_in_dim.23) | data formatting | bytes 12582912 | tf_op jit(solution)/shard_map/convert_element_type | solution.py:43
  28.2 9.5 %scatter_custom_fusion = bf16[320,6144]{1,0:T(8,128)(2,1)} fusion(s32[256]{0:T(256)S(1)} %bitcast.114, f32[256,6144]{1,0:T(8,128)} %convert_element_type.34, f32[256]{0:T(256)S(1)} %mul.54, bf16[]{:T(256)} %constant.5.clone.1), kind=kCustom, calls=%fused_computation.6 | custom fusion | flops 3145728 | bytes 10224642 | tf_op jit(solution)/shard_map/scatter | solution.py:47
  37.7 7.3 %all-to-all-start = ((bf16[8,40,6144]{2,1,0:T(8,128)(2,1)}), bf16[8,40,6144]{2,1,0:T(8,128)(2,1)}, u32[]{:S(2)}, u32[]{:S(2)}) async-start(bf16[8,40,6144]{2,1,0:T(8,128)(2,1)} %bitcast.108), calls=%async_computation | async-start | bytes 7864320 | tf_op jit(solution)/shard_map/all_to_all | solution.py:50
  45.0 3.3 broadcast_in_dim.24
  48.3 2.7 reshape.118
  51.0 8.4 %scatter_custom_fusion.1 = bf16[320,6144]{1,0:T(8,128)(2,1)} fusion(s32[256]{0:T(256)S(1)} %bitcast.115, bf16[256,6144]{1,0:T(8,128)(2,1)} %reshape.118, bf16[]{:T(256)} %constant.5.clone.1), kind=kCustom, calls=%fused_computation.23 | custom fusion | bytes 3932672 | tf_op jit(solution)/shard_map/scatter | solution.py:46
  59.5 42.4 %all-to-all-done = bf16[8,40,6144]{2,1,0:T(8,128)(2,1)} async-done(((bf16[8,40,6144]{2,1,0:T(8,128)(2,1)}), bf16[8,40,6144]{2,1,0:T(8,128)(2,1)}, u32[]{:S(2)}, u32[]{:S(2)}) %all-to-all-start) | async-done | bytes 3932192 | tf_op jit(solution)/shard_map/all_to_all | solution.py:50
  101.9 6.4 %all-to-all-start.1 = ((bf16[8,40,6144]{2,1,0:T(8,128)(2,1)}), bf16[8,40,6144]{2,1,0:T(8,128)(2,1)}, u32[]{:S(2)}, u32[]{:S(2)}) async-start(bf16[8,40,6144]{2,1,0:T(8,128)(2,1)} %bitcast.107), calls=%async_computation.1 | async-start | bytes 7864320 | tf_op jit(solution)/shard_map/all_to_all | solution.py:49
  108.5 4.4 %fusion.2 = f32[320,256]{1,0:T(8,128)S(1)} fusion(bf16[320,6144]{1,0:T(8,128)(2,1)} %bitcast.5, bf16[1,256,6144]{2,1,0:T(8,128)(2,1)} %all-gather.9.cloned.1.call-done), kind=kOutput, calls=%fused_computation.7 | convolution fusion | flops 1006632960 | bytes 7405568 | tf_op jit(solution)/shard_map/dot_general | solution.py:28
  112.9 47.6 %all-to-all-done.1 = bf16[8,40,6144]{2,1,0:T(8,128)(2,1)} async-done(((bf16[8,40,6144]{2,1,0:T(8,128)(2,1)}), bf16[8,40,6144]{2,1,0:T(8,128)(2,1)}, u32[]{:S(2)}, u32[]{:S(2)}) %all-to-all-start.1) | async-done | bytes 3932192 | tf_op jit(solution)/shard_map/all_to_all | solution.py:49
  160.5 4.4 %fusion.7 = f32[320,256]{1,0:T(8,128)S(1)} fusion(bf16[320,6144]{1,0:T(8,128)(2,1)} %bitcast.8, bf16[6144,512]{1,0:T(8,128)(2,1)} %all-gather.5.cloned.1.call-done), kind=kOutput, calls=%fused_computation.12 | convolution fusion | flops 1006632960 | bytes 7405568 | tf_op jit(solution)/shard_map/dot_general | solution.py:55
  165.4 3.3 multiply_convert_fusion.2
  168.7 0.8 pad_maximum_fusion
  169.6 1.7 fusion.46
  171.2 1.7 fusion.45
  172.9 1.7 fusion.44
  174.6 1.7 fusion.43
  176.2 1.7 fusion.42
  177.9 1.7 fusion.41
  179.6 1.7 fusion.40
  181.2 1.7 fusion.39
  182.9 1.7 fusion.38
  184.6 1.7 fusion.37
  186.3 1.7 fusion.36
  188.0 1.7 fusion.35
  189.6 1.7 fusion.34
  191.4 1.7 fusion.33
  193.1 1.7 fusion.32
  194.7 1.7 fusion.31
  196.4 8.4 %all-to-all-start.3 = ((bf16[16,320,384]{2,1,0:T(8,128)(2,1)}), bf16[16,320,384]{2,1,0:T(8,128)(2,1)}, u32[]{:S(2)}, u32[]{:S(2)}) async-start(bf16[16,320,384]{2,1,0:T(8,128)(2,1)} %fusion.31), calls=%async_computation.3 | async-start | bytes 7864320 | tf_op jit(solution)/shard_map/all_to_all | solution.py:10
  204.8 3.3 fusion.5
  208.2 3.2 fusion
  211.4 63.0 %all-to-all-done.3 = bf16[16,320,384]{2,1,0:T(8,128)(2,1)} async-done(((bf16[16,320,384]{2,1,0:T(8,128)(2,1)}), bf16[16,320,384]{2,1,0:T(8,128)(2,1)}, u32[]{:S(2)}, u32[]{:S(2)}) %all-to-all-start.3) | async-done | bytes 3932192 | tf_op jit(solution)/shard_map/all_to_all | solution.py:10
  274.4 5.2 %all-to-all-start.2 = ((bf16[8,40,6144]{2,1,0:T(8,128)(2,1)}), bf16[8,40,6144]{2,1,0:T(8,128)(2,1)}, u32[]{:S(2)}, u32[]{:S(2)}) async-start(bf16[8,40,6144]{2,1,0:T(8,128)(2,1)} %bitcast.106), calls=%async_computation.2 | async-start | bytes 7864320 | tf_op jit(solution)/shard_map/all_to_all | solution.py:68
  279.6 3.0 copy.25
  282.6 2.8 copy.24
  285.4 51.3 %all-to-all-done.2 = bf16[8,40,6144]{2,1,0:T(8,128)(2,1)} async-done(((bf16[8,40,6144]{2,1,0:T(8,128)(2,1)}), bf16[8,40,6144]{2,1,0:T(8,128)(2,1)}, u32[]{:S(2)}, u32[]{:S(2)}) %all-to-all-start.2) | async-done | bytes 3932192 | tf_op jit(solution)/shard_map/all_to_all | solution.py:68
  336.7 7.3 %all-to-all-start.4 = ((bf16[320,16,384]{2,0,1:T(8,128)(2,1)}), bf16[320,16,384]{2,0,1:T(8,128)(2,1)}, u32[]{:S(2)}, u32[]{:S(2)}) async-start(bf16[320,16,384]{2,0,1:T(8,128)(2,1)} %copy.24), calls=%async_computation.4 | async-start | bytes 7864320 | tf_op jit(solution)/shard_map/all_to_all | solution.py:75
  344.1 9.7 %gather_fusion = bf16[256,6144]{1,0:T(8,128)(2,1)} fusion(bf16[320,6144]{1,0:T(8,128)(2,1)} %bitcast.12, s32[1024]{0:T(1024)S(1)} %pad_clamp_fusion), kind=kCustom, calls=%fused_computation | custom fusion | bytes 6292480 | tf_op jit(solution)/shard_map/gather | solution.py:71
  353.8 6.2 %reshape.96 = bf16[128,2,6144]{2,1,0:T(2,128)(2,1)S(1)} reshape(bf16[256,6144]{1,0:T(8,128)(2,1)} %gather_fusion) | data formatting | bytes 6291456 | tf_op jit(solution)/shard_map/reshape | solution.py:71
  360.0 9.7 %reduce_sum.25 = bf16[128,6144]{1,0:T(8,128)(2,1)} reduce(bf16[128,2,6144]{2,1,0:T(2,128)(2,1)S(1)} %reshape.96, bf16[]{:T(256)} %constant.5.clone.1), dimensions={1}, to_apply=%region_5.6 | reduce | flops 786432 | bytes 4718594 | tf_op jit(solution)/shard_map/reduce_sum | solution.py:72
  369.7 4.9 %fusion.21 = f32[1,384,256]{2,1,0:T(8,128)} fusion(bf16[5120,384]{1,0:T(8,128)(2,1)} %bitcast.29, bf16[5120,768]{1,0:T(8,128)(2,1)} %all-gather.7.cloned.1.call-done), kind=kOutput, calls=%fused_computation.26 | convolution fusion | flops 1006632960 | bytes 6946816 | tf_op jit(solution)/shard_map/dot_general | solution.py:22
  374.6 4.9 %fusion.24 = f32[1,384,256]{2,1,0:T(8,128)} fusion(bf16[5120,384]{1,0:T(8,128)(2,1)} %bitcast.29, bf16[5120,768]{1,0:T(8,128)(2,1)} %all-gather.7.cloned.1.call-done), kind=kOutput, calls=%fused_computation.27 | convolution fusion | flops 1006632960 | bytes 6946816 | tf_op jit(solution)/shard_map/dot_general | solution.py:22
  379.5 19.6 %all-to-all-done.4 = bf16[320,16,384]{2,0,1:T(8,128)(2,1)} async-done(((bf16[320,16,384]{2,0,1:T(8,128)(2,1)}), bf16[320,16,384]{2,0,1:T(8,128)(2,1)}, u32[]{:S(2)}, u32[]{:S(2)}) %all-to-all-start.4) | async-done | bytes 3932192 | tf_op jit(solution)/shard_map/all_to_all | solution.py:75
  399.1 5.2 %fusion.27 = f32[1,256,384]{2,1,0:T(8,128)} fusion(bf16[5120,384]{1,0:T(8,128)(2,1)} %bitcast.33, bf16[5120,768]{1,0:T(8,128)(2,1)} %all-gather.7.cloned.1.call-done), kind=kOutput, calls=%fused_computation.28 | convolution fusion | flops 1006632960 | bytes 6946816 | tf_op jit(solution)/shard_map/dot_general | solution.py:22
  (33 shorter events, 3.9 us)
Async XLA Ops:
  7.2 101.3 %all-gather.9.cloned.1.call-start = ((), (), s32[]{:S(2)}) async-start(), calls=%async_computation.7 | async-start | bytes 3342336 | tf_op jit(solution)/shard_map/all_gather | solution.py:57
  7.9 152.6 %all-gather.5.cloned.1.call-start = ((), (), s32[]{:S(2)}) async-start(), calls=%async_computation.5 | async-start | bytes 6684672 | tf_op jit(solution)/shard_map/all_gather | solution.py:17
  19.5 8.4 %copy-start.1 = (f32[128,2]{0,1:T(2,128)S(1)}, f32[128,2]{0,1:T(2,128)}, u32[]{:S(2)}) copy-start(f32[128,2]{0,1:T(2,128)} %param.10) | copy-start | bytes 3076
  37.7 64.2 %all-to-all-start = ((bf16[8,40,6144]{2,1,0:T(8,128)(2,1)}), bf16[8,40,6144]{2,1,0:T(8,128)(2,1)}, u32[]{:S(2)}, u32[]{:S(2)}) async-start(bf16[8,40,6144]{2,1,0:T(8,128)(2,1)} %bitcast.108), calls=%async_computation | async-start | bytes 7864320 | tf_op jit(solution)/shard_map/all_to_all | solution.py:50
  101.9 58.6 %all-to-all-start.1 = ((bf16[8,40,6144]{2,1,0:T(8,128)(2,1)}), bf16[8,40,6144]{2,1,0:T(8,128)(2,1)}, u32[]{:S(2)}, u32[]{:S(2)}) async-start(bf16[8,40,6144]{2,1,0:T(8,128)(2,1)} %bitcast.107), calls=%async_computation.1 | async-start | bytes 7864320 | tf_op jit(solution)/shard_map/all_to_all | solution.py:49
  108.3 261.5 %all-gather.7.cloned.1.call-start = ((), (), s32[]{:S(2)}) async-start(), calls=%async_computation.6 | async-start | bytes 8355840 | tf_op jit(solution)/shard_map/all_gather | solution.py:17
  160.5 4.9 %copy-start = (bf16[6144,512]{1,0:T(8,128)(2,1)S(1)}, bf16[6144,512]{1,0:T(8,128)(2,1)}, u32[]{:S(2)}) copy-start(bf16[6144,512]{1,0:T(8,128)(2,1)} %all-gather.5.cloned.1.call-done) | copy-start | bytes 18874372
  196.4 11.7 %slice-start = ((s8[6291456]{0:T(1024)(128)(4,1)}), s8[2097152]{0:T(1024)(128)(4,1)S(1)}, s32[]{:S(2)}) async-start(s8[6291456]{0:T(1024)(128)(4,1)} %bitcast.110), calls=%async_computation.8 | async-start | bytes 4194304
  196.4 78.0 %all-to-all-start.3 = ((bf16[16,320,384]{2,1,0:T(8,128)(2,1)}), bf16[16,320,384]{2,1,0:T(8,128)(2,1)}, u32[]{:S(2)}, u32[]{:S(2)}) async-start(bf16[16,320,384]{2,1,0:T(8,128)(2,1)} %fusion.31), calls=%async_computation.3 | async-start | bytes 7864320 | tf_op jit(solution)/shard_map/all_to_all | solution.py:10
  204.8 3.4 slice-start.1
  274.4 62.4 %all-to-all-start.2 = ((bf16[8,40,6144]{2,1,0:T(8,128)(2,1)}), bf16[8,40,6144]{2,1,0:T(8,128)(2,1)}, u32[]{:S(2)}, u32[]{:S(2)}) async-start(bf16[8,40,6144]{2,1,0:T(8,128)(2,1)} %bitcast.106), calls=%async_computation.2 | async-start | bytes 7864320 | tf_op jit(solution)/shard_map/all_to_all | solution.py:68
  336.7 62.3 %all-to-all-start.4 = ((bf16[320,16,384]{2,0,1:T(8,128)(2,1)}), bf16[320,16,384]{2,0,1:T(8,128)(2,1)}, u32[]{:S(2)}, u32[]{:S(2)}) async-start(bf16[320,16,384]{2,0,1:T(8,128)(2,1)} %copy.24), calls=%async_computation.4 | async-start | bytes 7864320 | tf_op jit(solution)/shard_map/all_to_all | solution.py:75
Sparse Core Ops, SparseCore 0:
  9.6 36.6 all-gather.8
  48.6 85.5 all-gather.4
  169.7 82.8 all-gather.6
